TPU v7x, 32 devices: a whole 2x2x4 slice. The times are simulated.
32 devices in a mesh: group: 8 (over z, y), local: 4 (over x, core).
Axes of the slice: x: 2, y: 2, z: 4, core: 2. Of those that a mesh axis runs over, the one named last changes fastest.
Arguments:
- dense_vec: bfloat16 [4096, 128], P(('group', 'local')), may hold values from -6 to 6
- q_tables: float32 [1024, 26, 128], P('group'), may hold values from -4 to 4
- r_tables: float32 [256, 26, 128], P('local'), may hold values from -4 to 4
- owner: int32 [4096, 26, 1], P(('group', 'local')), may hold values from 0 to 7; in each aligned block of 3328 rows (0 to 3327, 3328 to 6655, ..., all dimensions but the last counted through in order) at most 832 rows name the same one
- q_local: int32 [4096, 26], P(('group', 'local')), may hold values from 0 to 127
- r_index: int32 [4096, 26], P(('group', 'local')), may hold values from 0 to 255
- w_one: bfloat16 [479, 1024], replicated, may hold values from -0.25 to 0.25
- b_one: float32 [1024], replicated, may hold values from -3 to 3
- w_two: bfloat16 [1024, 1024], replicated, may hold values from -0.1875 to 0.1875
- b_two: float32 [1024], replicated, may hold values from -3 to 3
- w_three: bfloat16 [1024, 512], replicated, may hold values from -0.1875 to 0.1875
- b_three: float32 [512], replicated, may hold values from -3 to 3
- w_four: bfloat16 [512, 256], replicated, may hold values from -0.25 to 0.25
- b_four: float32 [256], replicated, may hold values from -3 to 3
- cotangent: bfloat16 [4096, 256], P(('group', 'local')), may hold values from -6 to 6
Outputs:
- q_new: float32 [1024, 26, 128], P('group')
- r_new: float32 [256, 26, 128], P('local')
- w_one_new: float32 [479, 1024], replicated
- b_one_new: float32 [1024], replicated
- w_two_new: float32 [1024, 1024], replicated
- b_two_new: float32 [1024], replicated
- w_three_new: float32 [1024, 512], replicated
- b_three_new: float32 [512], replicated
- w_four_new: float32 [512, 256], replicated
- b_four_new: float32 [256], replicated
Inputs may be any that keep to these rules, and one draw needn't show every extreme that they name: `owner`: within the rows of one device (its 128 samples times 26 tables), no group is named more than 832 times, a bound that some block reaches.
All inputs are finite; a program needn't handle non-finite values.
Results may differ from a plain program's by a relative error of at most 0.0025.
Values may be sent and summed in bfloat16 or wider, within the bound.
A program may use at most 128 MiB of HBM per device.

v0:
```python
import jax
import jax.numpy as jnp
import numpy as np
from jax import lax
from jax.sharding import PartitionSpec as P

table_rate = 0.05
dense_rate = 0.0005


def silu_slope(preact):
    sigma = jax.nn.sigmoid(preact)
    return sigma * (1.0 + preact * (1.0 - sigma))


def interact(dense_rows, embeds):
    vectors_all = jnp.concatenate([dense_rows[:, None, :], embeds], axis=1).astype(jnp.float32)
    gram_mat = jnp.einsum("bid,bjd->bij", vectors_all, vectors_all, precision=lax.Precision.HIGHEST)
    lower_i, lower_j = np.tril_indices(vectors_all.shape[1], -1)
    pair_vals = gram_mat[:, lower_i, lower_j]
    features = jnp.concatenate([dense_rows.astype(jnp.float32), pair_vals], axis=1).astype(
        jnp.bfloat16
    )
    return (vectors_all, features)


def pair_back(d_pairs, vectors_all):
    vectors = vectors_all.shape[1]
    lower_i, lower_j = np.tril_indices(vectors, -1)
    spread = (
        jnp.zeros((vectors_all.shape[0], vectors, vectors), jnp.float32)
        .at[:, lower_i, lower_j]
        .set(d_pairs)
    )
    spread = spread + jnp.swapaxes(spread, 1, 2)
    return jnp.einsum("bij,bjd->bid", spread, vectors_all, precision=lax.Precision.HIGHEST)


def contract_rows(left, right):
    return lax.dot_general(
        left, right, (((0,), (0,)), ((), ())), preferred_element_type=jnp.float32
    )


def dense_pass(features, layers, cot_rows):
    inputs_list = [features]
    pre_list = []
    current = features
    for layer_idx, (weight, biases) in enumerate(layers):
        pre_act = jnp.dot(current, weight, preferred_element_type=jnp.float32) + biases
        pre_list.append(pre_act)
        if layer_idx + 1 < len(layers):
            current = jax.nn.silu(pre_act).astype(jnp.bfloat16)
            inputs_list.append(current)
    grad_low = cot_rows
    grad_full = cot_rows.astype(jnp.float32)
    grads = []
    back_grad = None
    for layer_idx in reversed(range(len(layers))):
        weight = layers[layer_idx][0]
        w_grad = contract_rows(inputs_list[layer_idx], grad_low)
        b_grad = jnp.sum(grad_full, axis=0)
        back_grad = lax.dot_general(
            grad_low, weight, (((1,), (1,)), ((), ())), preferred_element_type=jnp.float32
        )
        grads.insert(0, (w_grad, b_grad))
        if layer_idx > 0:
            grad_full = back_grad * silu_slope(pre_list[layer_idx - 1])
            grad_low = grad_full.astype(jnp.bfloat16)
    return (grads, back_grad)


def body(
    dense_vec,
    q_tables,
    r_tables,
    owner,
    q_local,
    r_index,
    w_one,
    b_one,
    w_two,
    b_two,
    w_three,
    b_three,
    w_four,
    b_four,
    cotangent,
):
    layers = [(w_one, b_one), (w_two, b_two), (w_three, b_three), (w_four, b_four)]
    groups = lax.axis_size("group")
    batch_rows, table_count = q_local.shape
    embed_width = q_tables.shape[2]
    lookups = batch_rows * table_count
    capacity = 2 * lookups // groups
    slot_count = groups * capacity
    segment_count = q_tables.shape[0] * table_count
    table_ids = jnp.arange(table_count, dtype=jnp.int32)[None, :]
    highest = lax.Precision.HIGHEST
    dest_group = owner[:, :, 0]
    owner_hits = (
        dest_group[:, :, None] == jnp.arange(groups, dtype=jnp.int32)[None, None, :]
    ).astype(jnp.float32)
    table_lower = (jnp.arange(table_count)[:, None] < jnp.arange(table_count)[None, :]).astype(
        jnp.float32
    )
    sample_lower = (jnp.arange(batch_rows)[:, None] < jnp.arange(batch_rows)[None, :]).astype(
        jnp.float32
    )
    within = jnp.einsum("st,bsg->btg", table_lower, owner_hits, precision=highest)
    before = jnp.einsum("cb,cg->bg", sample_lower, jnp.sum(owner_hits, axis=1), precision=highest)
    slot_rank = jnp.sum((within + before[:, None, :]) * owner_hits, axis=2).astype(jnp.int32)
    position = (dest_group * capacity + slot_rank).reshape(lookups)
    source = (
        jnp.full((slot_count,), lookups, jnp.int32)
        .at[position]
        .set(jnp.arange(lookups, dtype=jnp.int32))
    )
    row_keys = (q_local * table_count + table_ids).reshape(lookups)
    keys_padded = jnp.concatenate([row_keys, jnp.zeros((1,), jnp.int32)])
    outgoing = keys_padded[source].reshape(groups, capacity)
    flat_table = q_tables.reshape(segment_count, embed_width)
    request = lax.all_to_all(outgoing, "group", split_axis=0, concat_axis=0, tiled=True)
    served_rows = flat_table[request].astype(jnp.bfloat16)
    arrived = lax.all_to_all(served_rows, "group", split_axis=0, concat_axis=0, tiled=True)
    q_rows = arrived.reshape(slot_count, embed_width)[position]
    full_r = lax.all_gather(r_tables, "local", axis=0, tiled=True)
    remainder_count = full_r.shape[0]
    r_pick = (
        r_index[:, :, None] == jnp.arange(remainder_count, dtype=jnp.int32)[None, None, :]
    ).astype(jnp.float32)
    r_rows = jnp.einsum("btr,rtd->btd", r_pick, full_r, precision=highest).reshape(
        lookups, embed_width
    )
    q_val = q_rows.astype(jnp.float32)
    embeds = (q_val * r_rows).astype(jnp.bfloat16).reshape(batch_rows, table_count, embed_width)
    vectors_all, features = interact(dense_vec, embeds)
    grads, d_features = dense_pass(features, layers, cotangent)
    d_embed = pair_back(d_features[:, embed_width:], vectors_all)[:, 1:, :].reshape(
        lookups, embed_width
    )
    grad_padded = jnp.concatenate(
        [d_embed * r_rows, jnp.zeros((1, embed_width), jnp.float32)], axis=0
    )
    outbound = grad_padded[source].reshape(groups, capacity, embed_width)
    returned = (
        lax.all_to_all(
            outbound.astype(jnp.bfloat16), "group", split_axis=0, concat_axis=0, tiled=True
        )
        .astype(outbound.dtype)
        .reshape(slot_count, embed_width)
    )
    served_flat = request.reshape(slot_count)
    q_part = jax.ops.segment_sum(returned, served_flat, num_segments=segment_count).reshape(
        q_tables.shape
    )
    q_piece = lax.psum_scatter(
        q_part.astype(jnp.bfloat16), "local", scatter_dimension=0, tiled=True
    ).astype(jnp.float32)
    quarter = q_piece.shape[0]
    own_rows = lax.dynamic_slice_in_dim(q_tables, lax.axis_index("local") * quarter, quarter, 0)
    q_new = lax.all_gather(own_rows - table_rate * q_piece, "local", axis=0, tiled=True)
    r_part = jnp.einsum(
        "btr,btd->rtd",
        r_pick,
        (d_embed * q_val).reshape(batch_rows, table_count, embed_width),
        precision=highest,
    )
    summed = lax.psum(r_part, ("group", "local"))
    r_grad = lax.dynamic_slice_in_dim(
        summed, lax.axis_index("local") * r_tables.shape[0], r_tables.shape[0], 0
    )
    r_new = r_tables - table_rate * r_grad
    grad_wa, grad_ba, grad_wb, grad_bb, grad_wc, grad_bc, grad_wd, grad_bd = lax.psum(
        (
            grads[0][0],
            grads[0][1],
            grads[1][0],
            grads[1][1],
            grads[2][0],
            grads[2][1],
            grads[3][0],
            grads[3][1],
        ),
        ("group", "local"),
    )
    summed_grads = [(grad_wa, grad_ba), (grad_wb, grad_bb), (grad_wc, grad_bc), (grad_wd, grad_bd)]
    updated = []
    for (weight, biases), (w_grad, b_grad) in zip(layers, summed_grads):
        updated.append(weight.astype(jnp.float32) - dense_rate * w_grad)
        updated.append(biases - dense_rate * b_grad)
    return (
        q_new,
        r_new,
        updated[0],
        updated[1],
        updated[2],
        updated[3],
        updated[4],
        updated[5],
        updated[6],
        updated[7],
    )


def solution(mesh):
    return jax.shard_map(
        body,
        mesh=mesh,
        in_specs=(
            P(("group", "local"), None),
            P("group", None, None),
            P("local", None, None),
            P(("group", "local"), None, None),
            P(("group", "local"), None),
            P(("group", "local"), None),
            P(),
            P(),
            P(),
            P(),
            P(),
            P(),
            P(),
            P(),
            P(("group", "local"), None),
        ),
        out_specs=(
            P("group", None, None),
            P("local", None, None),
            P(),
            P(),
            P(),
            P(),
            P(),
            P(),
            P(),
            P(),
        ),
        check_vma=False,
    )
```

profile of v0, /device:TPU:0, one launch (start us, length us, event | category | flops | bytes accessed | tf_op | source)
XLA Modules:
  0.0 590.5 jit_solution(14401636984354006459)
XLA Ops:
  11.3 12.8 %scatter_custom_fusion = s32[6656]{0:T(1024)S(1)} fusion(s32[3328]{0:T(1024)S(1)} %fusion.38, s32[3328]{0:T(1024)S(1)} %iota.29, s32[]{:T(128)} %constant.27.clone.1), kind=kCustom, calls=%fused_computation.84 | custom fusion | bytes 26628 | tf_op jit(solution)/shard_map/scatter | solution.py:117
  24.1 34.5 %gather_fusion = s32[6656]{0:T(1024)S(1)} fusion(s32[3329]{0:T(1024)S(1)} %pad_add_fusion, s32[7168]{0:T(1024)S(1)} %pad_clamp_fusion.1), kind=kCustom, calls=%fused_computation | custom fusion | bytes 79872 | tf_op jit(solution)/shard_map/gather | solution.py:121
  59.4 7.3 %all-to-all-start = ((s32[8,1,832]{2,1,0:T(1,128)}), s32[8,1,832]{2,1,0:T(1,128)S(1)}, u32[]{:S(2)}, u32[]{:S(2)}) async-start(s32[8,1,832]{2,1,0:T(1,128)} %all_to_all.14), calls=%async_computation | async-start | bytes 57344 | tf_op jit(solution)/shard_map/all_to_all | solution.py:123
  66.7 2.5 copy.64
  69.4 4.0 all-to-all-done
  73.5 14.3 %gather_fusion.1 = bf16[6656,128]{1,0:T(8,128)(2,1)} fusion(bf16[3328,128]{1,0:T(8,128)(2,1)S(1)} %reshape.127, s32[7168]{0:T(1024)S(1)} %pad_clamp_fusion), kind=kCustom, calls=%fused_computation.1 | custom fusion | bytes 3434496 | tf_op jit(solution)/shard_map/gather | solution.py:124
  87.8 3.8 all-to-all-start.1
  91.7 38.3 %all-to-all-done.1 = bf16[8,832,128]{2,1,0:T(8,128)(2,1)S(1)} async-done(((bf16[8,832,128]{2,1,0:T(8,128)(2,1)}), bf16[8,832,128]{2,1,0:T(8,128)(2,1)S(1)}, u32[]{:S(2)}, u32[]{:S(2)}) %all-to-all-start.1) | async-done | bytes 1703968 | tf_op jit(solution)/shard_map/all_to_all | solution.py:125
  130.0 6.5 %gather_fusion.2 = bf16[3328,128]{1,0:T(8,128)(2,1)S(1)} fusion(bf16[6656,128]{1,0:T(8,128)(2,1)S(1)} %bitcast.53, s32[4096]{0:T(1024)S(1)} %pad_clamp_fusion.2), kind=kCustom, calls=%fused_computation.2 | custom fusion | bytes 1717248 | tf_op jit(solution)/shard_map/gather | solution.py:126
  137.2 7.3 %fusion.5 = (bf16[128,26,128]{2,0,1:T(8,128)(2,1)S(1)}, f32[26,128,128]{2,1,0:T(8,128)}) fusion(f32[128,26,128]{2,1,0:T(8,128)S(1)} %reshape.131, f32[256,26,128]{2,0,1:T(8,128)} %all-gather.3.cloned.1.call-done, s32[128,26]{0,1:T(8,128)S(1)} %copy-done.28), kind=kOutput, calls=%fused_computation.19 | convolution fusion | flops 1310326784 | bytes 7681024 | tf_op jit(solution)/shard_map/btr,rtd->btd/dot_general | solution.py:132
  145.3 1.1 copy.72
  146.4 4.9 gather_fusion.3
  151.3 1.5 convolution_add_fusion
  152.9 2.3 convolution_add_fusion.1
  156.3 0.8 fusion.44
  157.1 1.1 fusion.43
  158.8 1.5 fusion.42
  160.7 19.0 %scatter_fusion = f32[128,27,27]{0,2,1:T(8,128)S(1)} fusion(f32[128,27,27]{0,2,1:T(8,128)S(1)} %broadcast_in_dim.21, s32[351]{0:T(512)S(1)} %copy-done, f32[351,128]{1,0:T(8,128)S(1)} %convolution_bitcast_fusion), kind=kCustom, calls=%fused_computation.6 | custom fusion | bytes 541944 | tf_op jit(solution)/shard_map/scatter | solution.py:33
  180.0 2.9 copy.87
  182.9 3.3 fusion.14
  186.2 1.1 bitcast_multiply_fusion
  187.9 1.1 mul.158
  189.0 1.2 concatenate.24
  190.2 15.5 %gather_fusion.4 = bf16[6656,128]{1,0:T(8,128)(2,1)} fusion(bf16[3329,128]{1,0:T(8,128)(2,1)S(1)} %concatenate.24, s32[7168]{0:T(1024)} %copy-done.22), kind=kCustom, calls=%fused_computation.4 | custom fusion | bytes 3434496 | tf_op jit(solution)/shard_map/gather | solution.py:145
  205.7 4.4 all-to-all-start.2
  210.3 39.2 %all-to-all-done.2 = bf16[8,832,128]{2,1,0:T(8,128)(2,1)} async-done(((bf16[8,832,128]{2,1,0:T(8,128)(2,1)}), bf16[8,832,128]{2,1,0:T(8,128)(2,1)}, u32[]{:S(2)}, u32[]{:S(2)}) %all-to-all-start.2) | async-done | bytes 1703968 | tf_op jit(solution)/shard_map/all_to_all | solution.py:147
  249.5 40.3 %scatter_custom_fusion.2 = f32[3328,128]{1,0:T(8,128)} fusion(s32[6656]{0:T(1024)S(1)} %reshape.188, bf16[6656,128]{1,0:T(8,128)(2,1)} %bitcast.13, f32[]{:T(128)} %constant.24.clone.1), kind=kCustom, calls=%fused_computation.9 | custom fusion | flops 1703936 | bytes 3407876 | tf_op jit(solution)/shard_map/scatter-add | solution.py:154
  289.8 1.5 convert_element_type.101
  291.4 1.2 convert_element_type.102
  292.7 2.1 fusion.20
  294.8 1.7 fusion.21
  296.5 1.8 fusion.28
  298.3 2.8 fusion.24
  301.1 6.2 %fusion.4 = f32[256,26,128]{0,2,1:T(8,128)} fusion(s32[128,26]{0,1:T(8,128)S(1)} %copy-done.28, f32[128,26,128]{2,1,0:T(8,128)S(1)} %fusion.14, f32[128,26,128]{2,1,0:T(8,128)S(1)} %copy-done.2), kind=kOutput, calls=%fused_computation.16 | convolution fusion | flops 1309900800 | bytes 6829056 | tf_op jit(solution)/shard_map/btr,btd->rtd/dot_general | solution.py:163
  307.3 14.6 %reduce-scatter.2.cloned.1.call-done = bf16[32,26,128]{2,1,0:T(8,128)(2,1)} async-done(((bf16[128,26,128]{2,1,0:T(8,128)(2,1)}), bf16[32,26,128]{2,1,0:T(8,128)(2,1)}) %reduce-scatter.2.cloned.1.call-update) | async-done | bytes 213008 | tf_op jit(solution)/shard_map/reduce_scatter | solution.py:157
  321.9 1.2 multiply_subtract_fusion.5
  323.2 1.0 copy.79
  324.8 40.8 %all-reduce.1 = (f32[1024]{0:T(1024)S(1)}, f32[1024]{0:T(1024)S(1)}, f32[512]{0:T(512)S(1)}, f32[256]{0:T(256)S(1)}) all-reduce(f32[1024]{0:T(1024)S(1)} %copy-done.34, f32[1024]{0:T(1024)S(1)} %copy-done.33, f32[512]{0:T(512)S(1)} %copy-done.37, f32[256]{0:T(256)S(1)} %convert_reduce_fusion), channel_id=1, replica_groups=mesh['group'=8,'local'=4] {'group','local'}, use_global_device_ids=true, to_apply=%region_9.10 | all-reduce | flops 2816 | bytes 22528 | tf_op jit(solution)/shard_map/psum | solution.py:174
  367.4 192.2 %all-reduce.5.cloned.1.call-done = (f32[256,26,128]{0,2,1:T(8,128)}, f32[479,1024]{1,0:T(8,128)}, f32[1024,1024]{1,0:T(8,128)}, f32[1024,512]{1,0:T(8,128)}, f32[512,256]{1,0:T(8,128)}) async-done(((f32[256,26,128]{0,2,1:T(8,128)}, f32[479,1024]{1,0:T(8,128)}, f32[1024,1024]{1,0:T(8,128)}, f32[1024,512]{1,0:T(8,128)}, f32[512,256]{1,0:T(8,128)}), (f32[256,26,128]{0,2,1:T(8,128)}, f32[479,1024]{1,0:T(8,128)}, ...) | async-done | bytes 12185616 | tf_op jit(solution)/shard_map/psum | solution.py:169
  559.5 2.0 multiply_subtract_fusion.3
  561.5 1.4 copy.83
  562.9 1.9 multiply_subtract_fusion.4
  564.8 3.4 multiply_subtract_fusion.2
  568.2 1.7 multiply_subtract_fusion.1
  569.9 1.3 copy-done.5
  571.3 2.7 multiply_subtract_fusion
  574.0 7.2 %all-gather.5.cloned.1.call-done = f32[128,26,128]{2,0,1:T(8,128)} async-done(((f32[32,26,128]{2,0,1:T(8,128)}), f32[128,26,128]{2,0,1:T(8,128)}) %all-gather.5.cloned.1.call-update) | async-done | bytes 1703952 | tf_op jit(solution)/shard_map/all_gather | solution.py:162
  581.2 2.8 copy.112
  (129 shorter events, 12.4 us)
Async XLA Ops:
  7.2 129.6 %all-gather.3.cloned.1.call-start = ((), (), s32[]{:S(2)}) async-start(), calls=%async_computation.4 | async-start | bytes 4259840 | tf_op jit(solution)/shard_map/all_gather | solution.py:127
  24.1 34.6 %copy-start.22 = (s32[7168]{0:T(1024)}, s32[7168]{0:T(1024)S(1)}, u32[]{:S(2)}) copy-start(s32[7168]{0:T(1024)S(1)} %pad_clamp_fusion.1) | copy-start | bytes 86020
  59.4 14.0 %all-to-all-start = ((s32[8,1,832]{2,1,0:T(1,128)}), s32[8,1,832]{2,1,0:T(1,128)S(1)}, u32[]{:S(2)}, u32[]{:S(2)}) async-start(s32[8,1,832]{2,1,0:T(1,128)} %all_to_all.14), calls=%async_computation | async-start | bytes 57344 | tf_op jit(solution)/shard_map/all_to_all | solution.py:123
  69.1 18.6 %copy-start.3 = (f32[128,26,128]{2,1,0:T(8,128)}, f32[128,26,128]{2,1,0:T(8,128)S(1)}, u32[]{:S(2)}) copy-start(f32[128,26,128]{2,1,0:T(8,128)S(1)} %copy.64) | copy-start | bytes 5111812
  73.3 14.4 %copy-start.23 = (s32[8,1,832]{2,1,0:T(1,128)}, s32[8,1,832]{2,1,0:T(1,128)S(1)}, u32[]{:S(2)}) copy-start(s32[8,1,832]{2,1,0:T(1,128)S(1)} %all-to-all-done) | copy-start | bytes 79876
  87.8 3.8 copy-start.25
  87.8 42.2 %all-to-all-start.1 = ((bf16[8,832,128]{2,1,0:T(8,128)(2,1)}), bf16[8,832,128]{2,1,0:T(8,128)(2,1)S(1)}, u32[]{:S(2)}, u32[]{:S(2)}) async-start(bf16[8,832,128]{2,1,0:T(8,128)(2,1)} %bitcast.55), calls=%async_computation.1 | async-start | bytes 3407872 | tf_op jit(solution)/shard_map/all_to_all | solution.py:125
  136.5 0.7 copy-start.28
  136.7 7.8 %copy-start.1 = (f32[128,26,128]{2,1,0:T(8,128)}, f32[128,26,128]{2,1,0:T(8,128)S(1)}, u32[]{:S(2)}) copy-start(f32[128,26,128]{2,1,0:T(8,128)S(1)} %reshape.131) | copy-start | bytes 5111812
  144.6 1.8 copy-start
  144.6 6.7 %copy-start.31 = (f32[1024]{0:T(1024)S(1)}, f32[1024]{0:T(1024)}, u32[]{:S(2)}) copy-start(f32[1024]{0:T(1024)} %param.30) | copy-start | bytes 12292
  145.3 7.6 %copy-start.32 = (f32[1024]{0:T(1024)S(1)}, f32[1024]{0:T(1024)}, u32[]{:S(2)}) copy-start(f32[1024]{0:T(1024)} %param.32) | copy-start | bytes 12292
  152.8 5.4 copy-start.11
  152.8 2.3 copy-start.14
  152.9 2.3 copy-start.35
  155.2 2.0 copy-start.17
  155.2 1.1 copy-start.19
  155.2 1.1 copy-start.29
  156.3 1.9 copy-start.39
  157.1 3.1 copy-start.26
  157.1 1.6 copy-start.9
  158.8 1.5 copy-start.6
  160.3 19.4 %copy-start.20 = (bf16[128,1024]{1,0:T(8,128)(2,1)}, bf16[128,1024]{1,0:T(8,128)(2,1)S(1)}, u32[]{:S(2)}) copy-start(bf16[128,1024]{1,0:T(8,128)(2,1)S(1)} %get-tuple-element.52) | copy-start | bytes 786436
  182.9 3.3 copy-start.4
  205.7 4.5 copy-start.24
  205.7 43.8 %all-to-all-start.2 = ((bf16[8,832,128]{2,1,0:T(8,128)(2,1)}), bf16[8,832,128]{2,1,0:T(8,128)(2,1)}, u32[]{:S(2)}, u32[]{:S(2)}) async-start(bf16[8,832,128]{2,1,0:T(8,128)(2,1)} %bitcast.54), calls=%async_computation.2 | async-start | bytes 3407872 | tf_op jit(solution)/shard_map/all_to_all | solution.py:147
  210.1 111.8 %reduce-scatter.2.cloned.1.call-start = ((), (), s32[]{:S(2)}) async-start(), calls=%async_computation.5 | async-start | bytes 1310720 | tf_op jit(solution)/shard_map/reduce_scatter | solution.py:157
  291.4 1.3 copy-start.30
  292.6 2.2 copy-start.21
  292.6 3.9 copy-start.18
  292.6 3.9 copy-start.27
  292.6 266.9 %all-reduce.5.cloned.1.call-start = ((), (), s32[]{:S(2)}) async-start(), calls=%async_computation.7 | async-start | bytes 24379392 | tf_op jit(solution)/shard_map/psum | solution.py:169
  294.8 3.5 copy-start.12
  298.3 2.8 copy-start.2
  307.3 16.9 %copy-start.8 = (f32[64,26,128]{2,0,1:T(8,128)S(1)}, f32[64,26,128]{2,0,1:T(8,128)}, u32[]{:S(2)}) copy-start(f32[64,26,128]{2,0,1:T(8,128)} %param.25) | copy-start | bytes 2555908
  307.3 273.9 %all-gather.5.cloned.1.call-start = ((), (), s32[]{:S(2)}) async-start(), calls=%async_computation.6 | async-start | bytes 2129920 | tf_op jit(solution)/shard_map/all_gather | solution.py:162
  323.1 1.7 copy-start.33
  323.1 1.7 copy-start.34
  323.1 1.6 copy-start.37
  323.1 42.5 %copy-start.38 = (f32[256]{0:T(256)S(1)}, f32[256]{0:T(256)}, u32[]{:S(2)}) copy-start(f32[256]{0:T(256)} %param.36) | copy-start | bytes 3076
  323.2 43.0 %copy-start.36 = (f32[512]{0:T(512)S(1)}, f32[512]{0:T(512)}, u32[]{:S(2)}) copy-start(f32[512]{0:T(512)} %param.34) | copy-start | bytes 6148
  561.5 1.4 copy-start.16
  561.5 3.3 copy-start.7
  562.9 5.3 copy-start.15
  564.8 3.4 copy-start.13
  564.8 5.1 copy-start.10
  568.2 3.0 copy-start.5
Sparse Core Ops, SparseCore 0:
  9.5 32.7 all-gather.2
  292.7 29.1 reduce-scatter.1
  328.9 230.5 all-reduce.4
  561.5 19.5 all-gather.4
where the time goes:
time: 592 us; the launch traced here: 591 us
  waiting for transfers between devices  296 us (50%)
  local copies, waits for them, and re-layouts  130 us (22%)
  other arithmetic  59.6 us (10%)
  blocking collectives  40.8 us (7%)
  matrix products  34 us (6%)
  starting transfers between devices  15.7 us (3%)
  between operations  14.4 us (2%)
    psum x1, waiting for transfers between devices, body(): summed = lax.psum(r_part, ('group', 'local'))  192 us
    psum x1, blocking collectives, body(): lax.psum((grads[0][0], grads[0][1], grads[1][0], grads[1][1], grads[2][0]...  40.8 us
    scatter-add x1, other arithmetic, body(): jax.ops.segment_sum(returned, served_flat, num_segments=segment_count)  40.3 us
    all_to_all x1, waiting for transfers between devices, body(): lax.all_to_all(outbound.astype(jnp.bfloat16), 'group', split_axis=0, conc...  39.2 us
    all_to_all x1, waiting for transfers between devices, body(): lax.all_to_all(served_rows, 'group', split_axis=0, concat_axis=0, tiled=T...  38.3 us
    gather x1, local copies, waits for them, and re-layouts, body(): outgoing = keys_padded[source].reshape(groups, capacity)  34.5 us
    scatter x1, local copies, waits for them, and re-layouts, pair_back(): spread = jnp.zeros((vectors_all.shape[0], vectors, vectors), jnp.float32)...  19 us
    gather x1, local copies, waits for them, and re-layouts, body(): outbound = grad_padded[source].reshape(groups, capacity, embed_width)  15.5 us
  transfers between devices with their start and end apart: 7, of which 6 were waited for; matrix products, arithmetic and copies ran while one was open for 18% of the time, Pallas kernels for 0%

commit v1 on v0

--- a/solution.py
+++ b/solution.py
@@ -166,7 +166,7 @@
         (d_embed * q_val).reshape(batch_rows, table_count, embed_width),
         precision=highest,
     )
-    summed = lax.psum(r_part, ("group", "local"))
+    summed = lax.psum(lax.psum(r_part, "local"), "group")
     r_grad = lax.dynamic_slice_in_dim(
         summed, lax.axis_index("local") * r_tables.shape[0], r_tables.shape[0], 0
     )

time: 592 us -> 683 us (1.15)
  waiting for transfers between devices: 296 us -> 386 us
    psum x1 -> x3, waiting for transfers between devices: 192 us -> 272 us  [the longest x1 144 us: body(): lax.psum((grads[0][0], grads[0][1], grads[1][0], grads[1][1], grads[2][0]...]
    all_gather x1, waiting for transfers between devices: 7.17 us -> 18.1 us  [body(): lax.all_gather(own_rows - table_rate * q_piece, 'local', axis=0, tiled=True)]
    all_to_all x1, waiting for transfers between devices: 39.2 us -> 30.5 us  [body(): lax.all_to_all(outbound.astype(jnp.bfloat16), 'group', split_axis=0, conc...]
    reduce_scatter x1, waiting for transfers between devices: 14.6 us -> 21.6 us  [body(): lax.psum_scatter(q_part.astype(jnp.bfloat16), 'local', scatter_dimension=...]
    unnamed x87 -> x83, local copies, waits for them, and re-layouts: 14.2 us -> 14.8 us
  transfers between devices with their start and end apart: 7 -> 9, of which waited for: 6 -> 7; matrix products, arithmetic and copies ran while one was open for 18% -> 22% of each run, Pallas kernels for 0% -> 0%
where the time goes in v1:
time: 683 us; the launch traced here: 682 us
  waiting for transfers between devices  386 us (57%)
  local copies, waits for them, and re-layouts  131 us (19%)
  other arithmetic  59.9 us (9%)
  blocking collectives  41.2 us (6%)
  matrix products  33.6 us (5%)
  starting transfers between devices  15.8 us (2%)
  between operations  14.7 us (2%)
    psum x1, waiting for transfers between devices, body(): lax.psum((grads[0][0], grads[0][1], grads[1][0], grads[1][1], grads[2][0]...  144 us
    psum x2, waiting for transfers between devices, body(): summed = lax.psum(lax.psum(r_part, 'local'), 'group')  128 us
    psum x1, blocking collectives, body(): lax.psum((grads[0][0], grads[0][1], grads[1][0], grads[1][1], grads[2][0]...  41.2 us
    scatter-add x1, other arithmetic, body(): jax.ops.segment_sum(returned, served_flat, num_segments=segment_count)  39.7 us
    all_to_all x1, waiting for transfers between devices, body(): lax.all_to_all(served_rows, 'group', split_axis=0, concat_axis=0, tiled=T...  38.3 us
    gather x1, local copies, waits for them, and re-layouts, body(): outgoing = keys_padded[source].reshape(groups, capacity)  34.5 us
    all_to_all x1, waiting for transfers between devices, body(): lax.all_to_all(outbound.astype(jnp.bfloat16), 'group', split_axis=0, conc...  30.5 us
    reduce_scatter x1, waiting for transfers between devices, body(): lax.psum_scatter(q_part.astype(jnp.bfloat16), 'local', scatter_dimension=...  21.6 us
  transfers between devices with their start and end apart: 9, of which 7 were waited for; matrix products, arithmetic and copies ran while one was open for 22% of the time, Pallas kernels for 0%

profile of v1, /device:TPU:0, one launch (start us, length us, event | category | flops | bytes accessed | tf_op | source)
XLA Modules:
  0.0 682.2 jit_solution(12099447482446068399)
XLA Ops:
  11.3 12.8 %scatter_custom_fusion = s32[6656]{0:T(1024)S(1)} fusion(s32[3328]{0:T(1024)S(1)} %fusion.38, s32[3328]{0:T(1024)S(1)} %iota.29, s32[]{:T(128)} %constant.27.clone.1), kind=kCustom, calls=%fused_computation.84 | custom fusion | bytes 26628 | tf_op jit(solution)/shard_map/scatter | solution.py:117
  24.1 34.5 %gather_fusion = s32[6656]{0:T(1024)S(1)} fusion(s32[3329]{0:T(1024)S(1)} %pad_add_fusion, s32[7168]{0:T(1024)S(1)} %pad_clamp_fusion.1), kind=kCustom, calls=%fused_computation | custom fusion | bytes 79872 | tf_op jit(solution)/shard_map/gather | solution.py:121
  59.3 7.3 %all-to-all-start = ((s32[8,1,832]{2,1,0:T(1,128)}), s32[8,1,832]{2,1,0:T(1,128)S(1)}, u32[]{:S(2)}, u32[]{:S(2)}) async-start(s32[8,1,832]{2,1,0:T(1,128)} %all_to_all.14), calls=%async_computation | async-start | bytes 57344 | tf_op jit(solution)/shard_map/all_to_all | solution.py:123
  66.6 2.5 copy.64
  69.3 4.0 all-to-all-done
  73.5 14.3 %gather_fusion.1 = bf16[6656,128]{1,0:T(8,128)(2,1)} fusion(bf16[3328,128]{1,0:T(8,128)(2,1)S(1)} %reshape.127, s32[7168]{0:T(1024)S(1)} %pad_clamp_fusion), kind=kCustom, calls=%fused_computation.1 | custom fusion | bytes 3434496 | tf_op jit(solution)/shard_map/gather | solution.py:124
  87.7 3.8 all-to-all-start.1
  91.7 38.3 %all-to-all-done.1 = bf16[8,832,128]{2,1,0:T(8,128)(2,1)S(1)} async-done(((bf16[8,832,128]{2,1,0:T(8,128)(2,1)}), bf16[8,832,128]{2,1,0:T(8,128)(2,1)S(1)}, u32[]{:S(2)}, u32[]{:S(2)}) %all-to-all-start.1) | async-done | bytes 1703968 | tf_op jit(solution)/shard_map/all_to_all | solution.py:125
  129.9 6.5 gather_fusion.2
  137.2 7.3 %fusion.5 = (bf16[128,26,128]{2,0,1:T(8,128)(2,1)S(1)}, f32[26,128,128]{2,1,0:T(8,128)}) fusion(f32[128,26,128]{2,1,0:T(8,128)S(1)} %reshape.131, f32[256,26,128]{2,0,1:T(8,128)} %all-gather.3.cloned.1.call-done, s32[128,26]{0,1:T(8,128)S(1)} %copy-done.25), kind=kOutput, calls=%fused_computation.19 | convolution fusion | flops 1310326784 | bytes 7681024 | tf_op jit(solution)/shard_map/btr,rtd->btd/dot_general | solution.py:132
  145.3 1.1 copy.72
  146.4 4.9 gather_fusion.3
  151.7 2.3 convolution_add_fusion.1
  155.9 1.1 fusion.43
  157.6 1.5 fusion.42
  159.5 19.0 %scatter_fusion = f32[128,27,27]{0,2,1:T(8,128)S(1)} fusion(f32[128,27,27]{0,2,1:T(8,128)S(1)} %broadcast_in_dim.21, s32[351]{0:T(512)S(1)} %copy-done, f32[351,128]{1,0:T(8,128)S(1)} %convolution_bitcast_fusion), kind=kCustom, calls=%fused_computation.6 | custom fusion | bytes 541944 | tf_op jit(solution)/shard_map/scatter | solution.py:33
  178.8 2.9 copy.87
  181.7 3.3 fusion.14
  185.0 1.1 bitcast_multiply_fusion
  186.1 1.5 copy.78
  187.6 2.1 mul.158
  189.7 1.2 concatenate.24
  191.0 14.3 %gather_fusion.4 = bf16[6656,128]{1,0:T(8,128)(2,1)} fusion(bf16[3329,128]{1,0:T(8,128)(2,1)S(1)} %concatenate.24, s32[7168]{0:T(1024)S(1)} %pad_clamp_fusion.1), kind=kCustom, calls=%fused_computation.4 | custom fusion | bytes 3434496 | tf_op jit(solution)/shard_map/gather | solution.py:145
  205.2 4.4 all-to-all-start.2
  209.7 7.9 %fusion.4 = f32[256,26,128]{0,2,1:T(8,128)} fusion(s32[128,26]{0,1:T(8,128)S(1)} %copy-done.26, f32[128,26,128]{2,1,0:T(8,128)S(1)} %fusion.14, f32[128,26,128]{2,1,0:T(8,128)} %copy-done.1), kind=kOutput, calls=%fused_computation.16 | convolution fusion | flops 1309900800 | bytes 6829056 | tf_op jit(solution)/shard_map/btr,btd->rtd/dot_general | solution.py:163
  218.5 30.5 %all-to-all-done.2 = bf16[8,832,128]{2,1,0:T(8,128)(2,1)} async-done(((bf16[8,832,128]{2,1,0:T(8,128)(2,1)}), bf16[8,832,128]{2,1,0:T(8,128)(2,1)}, u32[]{:S(2)}, u32[]{:S(2)}) %all-to-all-start.2) | async-done | bytes 1703968 | tf_op jit(solution)/shard_map/all_to_all | solution.py:147
  249.0 39.7 %scatter_custom_fusion.2 = f32[3328,128]{1,0:T(8,128)S(1)} fusion(s32[6656]{0:T(1024)S(1)} %reshape.188, bf16[6656,128]{1,0:T(8,128)(2,1)} %bitcast.13, f32[]{:T(128)} %constant.24.clone.1), kind=kCustom, calls=%fused_computation.9 | custom fusion | flops 1703936 | bytes 3407876 | tf_op jit(solution)/shard_map/scatter-add | solution.py:154
  288.9 1.2 convert_element_type.102
  290.2 1.1 fusion.20
  291.3 1.7 fusion.21
  293.0 1.8 fusion.28
  294.8 2.8 fusion.24
  298.2 21.6 %reduce-scatter.2.cloned.1.call-done = bf16[32,26,128]{2,1,0:T(8,128)(2,1)} async-done(((bf16[128,26,128]{2,1,0:T(8,128)(2,1)}), bf16[32,26,128]{2,1,0:T(8,128)(2,1)}) %reduce-scatter.2.cloned.1.call-update) | async-done | bytes 213008 | tf_op jit(solution)/shard_map/reduce_scatter | solution.py:157
  319.9 1.2 multiply_subtract_fusion.5
  323.6 41.2 %all-reduce.1 = (f32[1024]{0:T(1024)S(1)}, f32[1024]{0:T(1024)S(1)}, f32[512]{0:T(512)S(1)}, f32[256]{0:T(256)S(1)}) all-reduce(f32[1024]{0:T(1024)S(1)} %copy-done.34, f32[1024]{0:T(1024)S(1)} %copy-done.33, f32[512]{0:T(512)} %get-tuple-element.54, ...), channel_id=1, replica_groups=mesh['group'=8,'local'=4] {'group','local'}, use_global_device_ids=true, to_apply=%region_10.11 | all-reduce | flops 2816 | bytes 22528 | tf_op jit(solution)/shard_map/psum | solution.py:174
  364.8 1.2 multiply_subtract_fusion.9
  366.0 1.3 multiply_subtract_fusion.8
  367.9 143.7 %all-reduce.11.cloned.1.call-done = (f32[479,1024]{1,0:T(8,128)}, f32[1024,1024]{1,0:T(8,128)}, f32[1024,512]{1,0:T(8,128)}, f32[512,256]{1,0:T(8,128)}) async-done(((f32[479,1024]{1,0:T(8,128)}, f32[1024,1024]{1,0:T(8,128)}, f32[1024,512]{1,0:T(8,128)}, f32[512,256]{1,0:T(8,128)}), (f32[479,1024]{1,0:T(8,128)}, f32[1024,1024]{1,0:T(8,128)}, f32[1024,512]{1,0:T(8,128)}, ...) | async-done | bytes 8777744 | tf_op jit(solution)/shard_map/psum | solution.py:174
  511.6 2.1 multiply_subtract_fusion.4
  513.7 3.4 multiply_subtract_fusion.2
  517.1 1.7 multiply_subtract_fusion.1
  518.7 1.3 copy-done.4
  520.0 2.7 multiply_subtract_fusion
  522.8 128.4 %all-reduce.9.cloned.1.call-done = f32[256,26,128]{0,2,1:T(8,128)} async-done(((f32[256,26,128]{0,2,1:T(8,128)}), f32[256,26,128]{0,2,1:T(8,128)}) %all-reduce.9.cloned.1.call-update) | async-done | bytes 3407888 | tf_op jit(solution)/shard_map/psum | solution.py:169
  651.1 2.0 multiply_subtract_fusion.3
  653.1 1.4 copy.83
  654.5 18.1 %all-gather.5.cloned.1.call-done = f32[128,26,128]{2,0,1:T(8,128)} async-done(((f32[32,26,128]{2,0,1:T(8,128)}), f32[128,26,128]{2,0,1:T(8,128)}) %all-gather.5.cloned.1.call-update) | async-done | bytes 1703952 | tf_op jit(solution)/shard_map/all_gather | solution.py:162
  672.5 2.8 copy.113
  (131 shorter events, 15.0 us)
Async XLA Ops:
  7.2 129.5 %all-gather.3.cloned.1.call-start = ((), (), s32[]{:S(2)}) async-start(), calls=%async_computation.4 | async-start | bytes 4259840 | tf_op jit(solution)/shard_map/all_gather | solution.py:127
  59.3 14.0 %all-to-all-start = ((s32[8,1,832]{2,1,0:T(1,128)}), s32[8,1,832]{2,1,0:T(1,128)S(1)}, u32[]{:S(2)}, u32[]{:S(2)}) async-start(s32[8,1,832]{2,1,0:T(1,128)} %all_to_all.14), calls=%async_computation | async-start | bytes 57344 | tf_op jit(solution)/shard_map/all_to_all | solution.py:123
  69.1 18.6 %copy-start.2 = (f32[128,26,128]{2,1,0:T(8,128)}, f32[128,26,128]{2,1,0:T(8,128)S(1)}, u32[]{:S(2)}) copy-start(f32[128,26,128]{2,1,0:T(8,128)S(1)} %copy.64) | copy-start | bytes 5111812
  73.3 14.4 %copy-start.20 = (s32[8,1,832]{2,1,0:T(1,128)}, s32[8,1,832]{2,1,0:T(1,128)S(1)}, u32[]{:S(2)}) copy-start(s32[8,1,832]{2,1,0:T(1,128)S(1)} %all-to-all-done) | copy-start | bytes 79876
  87.7 3.8 copy-start.22
  87.7 42.2 %all-to-all-start.1 = ((bf16[8,832,128]{2,1,0:T(8,128)(2,1)}), bf16[8,832,128]{2,1,0:T(8,128)(2,1)S(1)}, u32[]{:S(2)}, u32[]{:S(2)}) async-start(bf16[8,832,128]{2,1,0:T(8,128)(2,1)} %bitcast.55), calls=%async_computation.1 | async-start | bytes 3407872 | tf_op jit(solution)/shard_map/all_to_all | solution.py:125
  136.5 0.7 copy-start.25
  136.7 7.8 %copy-start.1 = (f32[128,26,128]{2,1,0:T(8,128)}, f32[128,26,128]{2,1,0:T(8,128)S(1)}, u32[]{:S(2)}) copy-start(f32[128,26,128]{2,1,0:T(8,128)S(1)} %reshape.131) | copy-start | bytes 5111812
  144.6 1.8 copy-start
  144.6 6.7 copy-start.5
  144.6 6.7 copy-start.29
  145.3 6.4 copy-start.31
  151.6 5.4 copy-start.10
  151.6 2.3 copy-start.13
  151.7 2.3 copy-start.35
  154.0 2.0 copy-start.15
  154.0 1.1 copy-start.17
  154.0 1.1 copy-start.27
  155.1 0.8 copy-start.36
  155.9 3.1 copy-start.23
  155.9 1.6 copy-start.8
  159.1 19.4 %copy-start.18 = (bf16[128,1024]{1,0:T(8,128)(2,1)}, bf16[128,1024]{1,0:T(8,128)(2,1)S(1)}, u32[]{:S(2)}) copy-start(bf16[128,1024]{1,0:T(8,128)(2,1)S(1)} %get-tuple-element.51) | copy-start | bytes 786436
  181.7 3.3 copy-start.3
  205.2 4.5 copy-start.26
  205.2 43.8 %all-to-all-start.2 = ((bf16[8,832,128]{2,1,0:T(8,128)(2,1)}), bf16[8,832,128]{2,1,0:T(8,128)(2,1)}, u32[]{:S(2)}, u32[]{:S(2)}) async-start(bf16[8,832,128]{2,1,0:T(8,128)(2,1)} %bitcast.54), calls=%async_computation.2 | async-start | bytes 3407872 | tf_op jit(solution)/shard_map/all_to_all | solution.py:147
  209.7 88.0 %all-reduce.7.cloned.1.call-start = ((), (), s32[]{:S(2)}) async-start(), calls=%async_computation.7 | async-start | bytes 6815744 | tf_op jit(solution)/shard_map/psum | solution.py:169
  217.7 0.7 copy-start.21
  217.7 102.2 %reduce-scatter.2.cloned.1.call-start = ((), (), s32[]{:S(2)}) async-start(), calls=%async_computation.5 | async-start | bytes 1310720 | tf_op jit(solution)/shard_map/reduce_scatter | solution.py:157
  288.9 1.3 copy-start.28
  288.9 1.3 copy-start.37
  288.9 2.4 copy-start.19
  290.1 2.9 copy-start.16
  290.1 2.9 copy-start.24
  290.1 221.5 %all-reduce.11.cloned.1.call-start = ((), (), s32[]{:S(2)}) async-start(), calls=%async_computation.9 | async-start | bytes 17563648 | tf_op jit(solution)/shard_map/psum | solution.py:174
  291.3 3.5 copy-start.11
  297.6 353.6 %all-reduce.9.cloned.1.call-start = ((), (), s32[]{:S(2)}) async-start(), calls=%async_computation.8 | async-start | bytes 6815744 | tf_op jit(solution)/shard_map/psum | solution.py:169
  298.2 24.0 %copy-start.7 = (f32[64,26,128]{2,0,1:T(8,128)S(1)}, f32[64,26,128]{2,0,1:T(8,128)}, u32[]{:S(2)}) copy-start(f32[64,26,128]{2,0,1:T(8,128)} %param.25) | copy-start | bytes 2555908
  298.2 374.4 %all-gather.5.cloned.1.call-start = ((), (), s32[]{:S(2)}) async-start(), calls=%async_computation.6 | async-start | bytes 2129920 | tf_op jit(solution)/shard_map/all_gather | solution.py:162
  321.1 2.5 copy-start.33
  321.1 2.5 copy-start.34
  321.1 46.2 %copy-start.30 = (f32[1024]{0:T(1024)S(1)}, f32[1024]{0:T(1024)}, u32[]{:S(2)}) copy-start(f32[1024]{0:T(1024)} %param.30) | copy-start | bytes 12292
  321.1 46.2 %copy-start.32 = (f32[1024]{0:T(1024)S(1)}, f32[1024]{0:T(1024)}, u32[]{:S(2)}) copy-start(f32[1024]{0:T(1024)} %param.32) | copy-start | bytes 12292
  322.2 191.5 %copy-start.6 = (bf16[479,1024]{1,0:T(8,128)(2,1)S(1)}, bf16[479,1024]{1,0:T(8,128)(2,1)}, u32[]{:S(2)}) copy-start(bf16[479,1024]{1,0:T(8,128)(2,1)} %param.29) | copy-start | bytes 2942980
  511.6 5.5 copy-start.14
  513.7 3.4 copy-start.12
  513.7 5.1 copy-start.9
  517.1 2.9 copy-start.4
Sparse Core Ops, SparseCore 0:
  9.5 32.7 all-gather.2
  217.8 73.9 all-reduce.6
  294.9 24.9 reduce-scatter.1
  326.6 184.9 all-reduce.10
  515.1 135.9 all-reduce.8
  653.1 19.3 all-gather.4
